TPU v7x, 32 devices: a whole 2x2x4 slice. The times are simulated.
32 devices in a mesh: seq: 8 (over y, x, core), batch: 4 (over z).
Axes of the slice: x: 2, y: 2, z: 4, core: 2. Of those that a mesh axis runs over, the one named last changes fastest.
Arguments:
- query_rows: bfloat16 [4, 1024, 2048], P('batch', 'seq'), may hold values from -6 to 6, as said below
- key_rows: bfloat16 [4, 1024, 1024], P('batch', 'seq'), may hold values from -6 to 6, as said below
- value_rows: bfloat16 [4, 1024, 1024], P('batch', 'seq'), may hold values from -6 to 6, as said below
- attn_output: bfloat16 [4, 1024, 2048], P('batch', 'seq'), may hold values from -6 to 6, as said below
- output_grad: bfloat16 [4, 1024, 2048], P('batch', 'seq'), may hold values from -6 to 6
- log_norm: float32 [4, 16, 1024], P('batch', None, 'seq'), as said below
- slab_order: int32 [4, 8], P('batch', 'seq'), may hold values from 0 to 7, as said below
- normed_input: bfloat16 [4, 1024, 4608], P('batch', 'seq'), may hold values from -6 to 6
Outputs:
- grad_query: bfloat16 [4, 1024, 2048], P('batch', 'seq')
- grad_key: bfloat16 [4, 1024, 1024], P('batch', 'seq')
- grad_weight: float32 [4608, 1024], P('seq')
Inputs may be any that keep to these rules, and one draw needn't show every extreme that they name: `query_rows`: queries of a causal forward pass with 16 heads. `key_rows`: keys of the same forward pass with 8 heads. `value_rows`: values of the same forward pass. `attn_output`: the forward pass's output: for each head, sum over keys at or before the query's position of exp(score - log_norm) times the value. `log_norm`: log of the sum of exp(score) over the keys at or before the query's position, so that each row's weights sum to one. `slab_order`: each row is a permutation of the slab places.
All inputs are finite; a program needn't handle non-finite values.
Results may differ from a plain program's by a relative error of at most 0.025.
Values may be sent and summed in bfloat16 or wider, within the bound.
A program may use at most 128 MiB of HBM per device.

v0:
```python
import jax
import jax.numpy as jnp
from jax import lax
from jax.sharding import PartitionSpec as P

HEADS = 16
KV_HEADS = 8
HEAD = 128
SCALE = 144.0 ** (-0.5)


def block_terms(queries, grads, delta, norms, query_pos, key_block, value_block, key_pos):
    keys_count = key_block.shape[0]
    scores = SCALE * jnp.einsum(
        "tgrd,kgd->grtk", queries, key_block, preferred_element_type=jnp.float32
    )
    allowed = key_pos[None, :] <= query_pos[:, None]
    probs = jnp.where(allowed, jnp.exp(scores - norms[..., None]), 0.0)
    dprob = jnp.einsum("tgrd,kgd->grtk", grads, value_block, preferred_element_type=jnp.float32)
    dscore = probs * (dprob - delta[..., None])
    probs_low = probs.astype(jnp.bfloat16)
    dscore_low = dscore.astype(jnp.bfloat16)
    grad_q = SCALE * jnp.einsum(
        "grtk,kgd->tgrd", dscore_low, key_block, preferred_element_type=jnp.float32
    )
    grad_k = SCALE * jnp.einsum(
        "grtk,tgrd->kgd", dscore_low, queries, preferred_element_type=jnp.float32
    )
    grad_v = jnp.einsum("grtk,tgrd->kgd", probs_low, grads, preferred_element_type=jnp.float32)
    return (grad_q, grad_k.reshape(keys_count, -1), grad_v.reshape(keys_count, -1))


def local(
    query_rows, key_rows, value_rows, attn_output, output_grad, log_norm, slab_order, normed_input
):
    tokens = query_rows.shape[1]
    group = HEADS // KV_HEADS
    kv_width = KV_HEADS * HEAD
    slabs = lax.axis_size("seq")
    length = tokens * slabs
    orders = lax.all_gather(slab_order, "seq", axis=1, tiled=True)
    queries = query_rows[0].reshape(tokens, KV_HEADS, group, HEAD)
    grads = output_grad[0].reshape(tokens, KV_HEADS, group, HEAD)
    outputs = attn_output[0].reshape(tokens, KV_HEADS, group, HEAD)
    delta = jnp.transpose(
        jnp.sum(grads.astype(jnp.float32) * outputs.astype(jnp.float32), axis=3), (1, 2, 0)
    )
    norms = log_norm[0].reshape(KV_HEADS, group, tokens)
    offsets = jnp.arange(tokens, dtype=jnp.int32)
    query_pos = slab_order[0, 0] * tokens + offsets
    width = tokens * -(-512 // tokens)
    empty_kv = jnp.zeros((length, kv_width), jnp.float32)
    empty_q = jnp.zeros((tokens, KV_HEADS, group, HEAD), jnp.float32)
    start = jnp.int32(0)
    grad_q = empty_q
    grad_k = empty_kv
    grad_v = empty_kv
    key_part = lax.all_gather(key_rows, "seq", axis=1, tiled=True)
    value_part = lax.all_gather(value_rows, "seq", axis=1, tiled=True)
    count = key_part.shape[1]
    for begin in range(0, count, width):
        finish = min(begin + width, count)
        shards = (finish - begin) // tokens
        first = (start + begin) // tokens
        places = lax.dynamic_slice_in_dim(orders[0], first, shards, 0)
        key_pos = (places[:, None] * tokens + offsets[None, :]).reshape(-1)
        key_block = key_part[0, begin:finish].reshape(-1, KV_HEADS, HEAD)
        value_block = value_part[0, begin:finish].reshape(-1, KV_HEADS, HEAD)
        term_q, term_k, term_v = block_terms(
            queries, grads, delta, norms, query_pos, key_block, value_block, key_pos
        )
        grad_q = grad_q + term_q
        grad_k = lax.dynamic_update_slice_in_dim(grad_k, term_k, begin, 0)
        grad_v = lax.dynamic_update_slice_in_dim(grad_v, term_v, begin, 0)
    grad_q, part_key, part_value = (grad_q, grad_k, grad_v)
    key_sum, value_sum = (
        lax.psum_scatter(
            part_key.astype(jnp.bfloat16), "seq", scatter_dimension=0, tiled=True
        ).astype(jnp.float32),
        lax.psum_scatter(
            part_value.astype(jnp.bfloat16), "seq", scatter_dimension=0, tiled=True
        ).astype(jnp.float32),
    )
    every_grad = lax.all_gather(value_sum.astype(jnp.bfloat16), "seq", axis=0, tiled=True)
    own_columns = lax.all_to_all(normed_input[0], "seq", split_axis=1, concat_axis=0, tiled=True)
    share = own_columns.shape[1]
    slab_parts = jnp.einsum(
        "std,stk->sdk",
        own_columns.reshape(slabs, tokens, share),
        every_grad.reshape(slabs, tokens, kv_width),
        preferred_element_type=jnp.float32,
    )
    rows_total = jnp.sum(slab_parts.astype(jnp.bfloat16).astype(jnp.float32), axis=0)
    weight = lax.psum(rows_total.astype(jnp.bfloat16), "batch").astype(jnp.float32)
    grad_query = grad_q.astype(jnp.bfloat16).reshape(1, tokens, HEADS * HEAD)
    grad_key = key_sum.astype(jnp.bfloat16).reshape(1, tokens, kv_width)
    return (grad_query, grad_key, weight)


def solution(mesh):
    placed = (
        P("batch", "seq", None),
        P("batch", "seq", None),
        P("batch", "seq", None),
        P("batch", "seq", None),
        P("batch", "seq", None),
        P("batch", None, "seq"),
        P("batch", "seq"),
        P("batch", "seq", None),
    )
    return jax.shard_map(
        local,
        mesh=mesh,
        in_specs=placed,
        out_specs=(P("batch", "seq", None), P("batch", "seq", None), P("seq", None)),
        check_vma=False,
    )
```

profile of v0, /device:TPU:0, one launch (start us, length us, event | category | flops | bytes accessed | tf_op | source)
XLA Modules:
  0.0 277.6 jit_solution(16221604361421081299)
XLA Ops:
  7.2 1.8 copy.57
  11.7 9.5 %all-reduce = s32[8]{0:T(128)S(1)} all-reduce(s32[8]{0:T(128)S(1)} %bitcast_dynamic-update-slice_fusion), channel_id=1, replica_groups=mesh['seq'=8,'batch'=4] {'seq'}, use_global_device_ids=true, to_apply=%add | all-reduce | flops 8 | bytes 64
  24.5 16.8 %all-gather.4.cloned.1.call-done = bf16[1,1024,1024]{1,2,0:T(8,128)(2,1)} async-done(((bf16[1,128,1024]{1,2,0:T(8,128)(2,1)}), bf16[1,1024,1024]{1,2,0:T(8,128)(2,1)}) %all-gather.4.cloned.1.call-update) | async-done | bytes 2097168 | tf_op jit(solution)/shard_map/all_gather | solution.py:58
  49.6 4.0 %copy.107 = bf16[1024,1024]{1,0:T(8,128)(2,1)} copy(bf16[1024,1024]{0,1:T(8,128)(2,1)} %pad_maximum_fusion.1) | data formatting | bytes 4194304
  54.6 40.3 %reduce-scatter.7.cloned.1.call-done = bf16[128,1024]{1,0:T(8,128)(2,1)} async-done(((bf16[1024,1024]{1,0:T(8,128)(2,1)}), bf16[128,1024]{1,0:T(8,128)(2,1)}) %reduce-scatter.7.cloned.1.call-update) | async-done | bytes 262160
  96.7 2.4 copy.81
  99.1 4.3 %all-to-all-start = ((bf16[128,8,576]{0,2,1:T(8,128)(2,1)}), bf16[128,8,576]{0,2,1:T(8,128)(2,1)}, u32[]{:S(2)}, u32[]{:S(2)}) async-start(bf16[128,8,576]{0,2,1:T(8,128)(2,1)} %bitcast.146), calls=%async_computation.1 | async-start | bytes 2359296 | tf_op jit(solution)/shard_map/all_to_all | solution.py:85
  103.5 3.1 %reshape.104 = f32[128,8,2,128]{3,2,1,0:T(2,128)} reshape(bf16[1,128,2048]{2,1,0:T(8,128)(2,1)} %param.11) | data formatting | bytes 1572864 | tf_op jit(solution)/shard_map/convert_element_type | solution.py:46
  106.6 3.2 %multiply_reduce_fusion = f32[128,8,2]{2,1,0:T(8,128)} fusion(f32[128,8,2,128]{3,2,1,0:T(2,128)} %reshape.104, bf16[128,8,2,128]{3,2,1,0:T(2,128)(2,1)S(1)} %reshape_squeeze.22), kind=kLoop, calls=%fused_computation.37 | loop fusion | flops 784384 | bytes 1581056 | tf_op jit(solution)/shard_map/reduce_sum | solution.py:46
  111.1 19.6 %all-gather.6.cloned.1.call-done = bf16[1,1024,1024]{1,2,0:T(8,128)(2,1)} async-done(((bf16[1,128,1024]{1,2,0:T(8,128)(2,1)}), bf16[1,1024,1024]{1,2,0:T(8,128)(2,1)}) %all-gather.6.cloned.1.call-update) | async-done | bytes 2097168 | tf_op jit(solution)/shard_map/all_gather | solution.py:59
  130.7 2.8 %fusion.35 = (bf16[1,512,1024]{1,2,0:T(8,128)(2,1)S(1)}, bf16[1,512,1024]{1,2,0:T(8,128)(2,1)}) fusion(bf16[1,1024,1024]{1,2,0:T(8,128)(2,1)} %all-gather.6.cloned.1.call-done), kind=kLoop, calls=%fused_computation.50 | loop fusion | bytes 4194304 | tf_op jit(solution)/shard_map/slice | solution.py:68
  133.6 2.9 %fusion.1 = bf16[8,2,128,512]{2,3,1,0:T(8,128)(2,1)} fusion(f32[8,512,128,2]{2,1,3,0:T(8,128)S(1)} %copy-done.4, bf16[512,8,128,1]{0,2,3,1:T(8,128)(2,1)S(1)} %bitcast.154, bf16[128,8,2,128]{0,3,2,1:T(8,128)(2,1)S(1)} %copy-done.7, f32[8,2,128]{2,1,0:T(2,128)S(1)} %copy.63, f32[8,2,128]{2,1,0:T(2,128)S(1)} %bitcast.161, ...), kind=kOutput, calls=%fused_computation.3 | convolution fusion | flops 274726912 | bytes 7946240 | tf_op jit(solution)/shard_map/tgrd,kgd->grtk/dot_general | solution.py:19
  136.5 24.1 %all-gather.8.cloned.1.call-done = bf16[1024,1024]{0,1:T(8,128)(2,1)} async-done(((bf16[128,1024]{0,1:T(8,128)(2,1)}), bf16[1024,1024]{0,1:T(8,128)(2,1)}) %all-gather.8.cloned.1.call-update) | async-done | bytes 2097168 | tf_op jit(solution)/shard_map/all_gather | solution.py:84
  160.6 3.9 %copy.80 = bf16[1024,1024]{1,0:T(8,128)(2,1)} copy(bf16[1024,1024]{0,1:T(8,128)(2,1)} %all-gather.8.cloned.1.call-done) | data formatting | bytes 4194304 | tf_op jit(solution)/shard_map/all_gather | solution.py:84
  164.5 5.8 %convert_reduce_fusion = bf16[1024,576]{0,1:T(8,128)(2,1)} fusion(bf16[8,128,1024]{2,1,0:T(8,128)(2,1)} %bitcast.150, bf16[128,8,576]{0,2,1:T(8,128)(2,1)} %all-to-all-done), kind=kOutput, calls=%fused_computation | convolution fusion | flops 1216806912 | bytes 4456448 | tf_op jit(solution)/shard_map/std,stk->sdk/dot_general | solution.py:87
  170.4 3.4 %fusion.14 = bf16[8,512,128]{1,2,0:T(8,128)(2,1)} fusion(bf16[8,2,128,512]{2,3,1,0:T(8,128)(2,1)} %fusion.1, bf16[128,8,2,128]{0,3,2,1:T(8,128)(2,1)S(1)} %bitcast.140), kind=kOutput, calls=%fused_computation.22 | convolution fusion | flops 269484032 | bytes 3670016 | tf_op jit(solution)/shard_map/grtk,tgrd->kgd/dot_general | solution.py:26
  173.8 2.3 copy.75
  176.1 4.0 %fusion.5 = bf16[8,2,128,512]{2,3,1,0:T(8,128)(2,1)S(1)} fusion(f32[8,512,128,2]{2,1,3,0:T(8,128)} %copy-done.2, bf16[512,8,128,1]{0,2,3,1:T(8,128)(2,1)} %bitcast.153, bf16[128,8,2,128]{0,3,2,1:T(8,128)(2,1)S(1)} %copy-done.7, f32[8,2,128]{2,1,0:T(2,128)S(1)} %copy.63, f32[8,2,128]{2,1,0:T(2,128)S(1)} %bitcast.162, pred[128,512]{0,1:T(8,128)(4,1)S(1)} %get-tuple-element.17), kind=kOutput, calls=%fused_computation.9 | convolution fusion | flops 274726912 | bytes 7946240 | tf_op jit(solution)/shard_map/tgrd,kgd->grtk/dot_general | solution.py:19
  181.9 2.3 copy.74
  184.2 3.1 %pad_maximum_fusion = bf16[1024,1024]{1,0:T(8,128)(2,1)} fusion(bf16[512,1024]{1,0:T(8,128)(2,1)} %copy.75, bf16[512,1024]{1,0:T(8,128)(2,1)} %copy.74), kind=kLoop, calls=%fused_computation.17 | loop fusion | flops 4194304 | bytes 4194304 | tf_op jit(solution)/shard_map/dynamic_update_slice | solution.py:73
  187.3 2.3 fusion.39
  191.1 35.4 %all-reduce.3.cloned.1.call-done = bf16[576,1024]{1,0:T(8,128)(2,1)} async-done(((bf16[576,1024]{1,0:T(8,128)(2,1)}), bf16[576,1024]{1,0:T(8,128)(2,1)}) %all-reduce.3.cloned.1.call-update) | async-done | bytes 1179664 | tf_op jit(solution)/shard_map/psum | solution.py:94
  226.5 3.0 %convert_element_type.60 = f32[576,1024]{1,0:T(8,128)} convert(bf16[576,1024]{1,0:T(8,128)(2,1)} %all-reduce.3.cloned.1.call-done) | non-fusion elementwise | flops 589824 | bytes 3538944 | tf_op jit(solution)/shard_map/convert_element_type | solution.py:94
  229.5 41.3 %reduce-scatter.5.cloned.1.call-done = bf16[128,1024]{1,0:T(8,128)(2,1)} async-done(((bf16[1024,1024]{1,0:T(8,128)(2,1)}), bf16[128,1024]{1,0:T(8,128)(2,1)}) %reduce-scatter.5.cloned.1.call-update) | async-done | bytes 262160 | tf_op jit(solution)/shard_map/reduce_scatter | solution.py:77
  (55 shorter events, 21.3 us)
Async XLA Ops:
  7.2 16.6 %copy-start.5 = (bf16[1,128,2048]{2,1,0:T(8,128)(2,1)S(1)}, bf16[1,128,2048]{2,1,0:T(8,128)(2,1)}, u32[]{:S(2)}) copy-start(bf16[1,128,2048]{2,1,0:T(8,128)(2,1)} %param.8) | copy-start | bytes 1572868
  7.2 34.1 %all-gather.4.cloned.1.call-start = ((), (), s32[]{:S(2)}) async-start(), calls=%async_computation.3 | async-start | bytes 2359296 | tf_op jit(solution)/shard_map/all_gather | solution.py:58
  9.1 85.8 %reduce-scatter.7.cloned.1.call-start = ((), (), s32[]{:S(2)}) async-start(), calls=%async_computation.8 | async-start | bytes 2359296
  43.7 2.0 copy-start.3
  43.8 2.0 copy-start.6
  43.8 2.0 copy-start.9
  44.5 2.4 copy-start.2
  49.6 4.1 %copy-start.8 = (bf16[1,128,1024]{2,1,0:T(8,128)(2,1)S(1)}, bf16[1,128,1024]{2,1,0:T(8,128)(2,1)}, u32[]{:S(2)}) copy-start(bf16[1,128,1024]{2,1,0:T(8,128)(2,1)} %param.10) | copy-start | bytes 786436
  53.6 77.1 %all-gather.6.cloned.1.call-start = ((), (), s32[]{:S(2)}) async-start(), calls=%async_computation.4 | async-start | bytes 2359296 | tf_op jit(solution)/shard_map/all_gather | solution.py:59
  54.5 106.0 %all-gather.8.cloned.1.call-start = ((), (), s32[]{:S(2)}) async-start(), calls=%async_computation.6 | async-start | bytes 2359296 | tf_op jit(solution)/shard_map/all_gather | solution.py:84
  99.1 65.4 %all-to-all-start = ((bf16[128,8,576]{0,2,1:T(8,128)(2,1)}), bf16[128,8,576]{0,2,1:T(8,128)(2,1)}, u32[]{:S(2)}, u32[]{:S(2)}) async-start(bf16[128,8,576]{0,2,1:T(8,128)(2,1)} %bitcast.146), calls=%async_computation.1 | async-start | bytes 2359296 | tf_op jit(solution)/shard_map/all_to_all | solution.py:85
  103.3 123.2 %all-reduce.3.cloned.1.call-start = ((), (), s32[]{:S(2)}) async-start(), calls=%async_computation.7 | async-start | bytes 2359296 | tf_op jit(solution)/shard_map/psum | solution.py:94
  109.9 23.7 %copy-start.7 = (bf16[128,8,2,128]{0,3,2,1:T(8,128)(2,1)S(1)}, bf16[128,8,2,128]{0,3,2,1:T(8,128)(2,1)}, u32[]{:S(2)}) copy-start(bf16[128,8,2,128]{0,3,2,1:T(8,128)(2,1)} %copy.77) | copy-start | bytes 1572868
  130.7 2.9 %copy-start.4 = (f32[8,512,128,2]{2,1,3,0:T(8,128)S(1)}, f32[8,512,128,2]{2,1,3,0:T(8,128)}, u32[]{:S(2)}) copy-start(f32[8,512,128,2]{2,1,3,0:T(8,128)} %copy-done.3) | copy-start | bytes 12582916
  170.4 100.4 %reduce-scatter.5.cloned.1.call-start = ((), (), s32[]{:S(2)}) async-start(), calls=%async_computation.5 | async-start | bytes 2359296 | tf_op jit(solution)/shard_map/reduce_scatter | solution.py:77
  180.0 1.8 copy-start.1
  187.3 2.3 copy-start
Sparse Core Ops, SparseCore 0:
  10.4 30.8 all-gather.3
  53.7 41.0 reduce-scatter.6
  97.3 33.3 all-gather.5
  132.4 28.0 all-gather.7
  170.5 55.9 all-reduce.2
  230.2 40.5 reduce-scatter.4
where the time goes:
time: 278 us
  waiting for transfers between devices  178 us (64%)
  local copies, waits for them, and re-layouts  35.5 us (13%)
  matrix products  24.2 us (9%)
  between operations  14.9 us (5%)
  other arithmetic  11.3 us (4%)
  blocking collectives  9.51 us (3%)
  starting transfers between devices  4.68 us (2%)
    reduce_scatter x1, waiting for transfers between devices, local(): lax.psum_scatter(part_key.astype(jnp.bfloat16), 'seq', scatter_dimension=...  41.3 us
    unnamed x7, waiting for transfers between devices  40.4 us
    psum x1, waiting for transfers between devices, local(): lax.psum(rows_total.astype(jnp.bfloat16), 'batch').astype(jnp.float32)  35.4 us
    all_gather x1, waiting for transfers between devices, local(): lax.all_gather(value_sum.astype(jnp.bfloat16), 'seq', axis=0, tiled=True)  24.1 us
    all_gather x1, waiting for transfers between devices, local(): value_part = lax.all_gather(value_rows, 'seq', axis=1, tiled=True)  19.6 us
    all_gather x1, waiting for transfers between devices, local(): key_part = lax.all_gather(key_rows, 'seq', axis=1, tiled=True)  16.8 us
    unnamed x29, local copies, waits for them, and re-layouts  15.3 us
    unnamed x1, blocking collectives  9.51 us
  transfers between devices with their start and end apart: 7, of which 6 were waited for; matrix products, arithmetic and copies ran while one was open for 18% of the time, Pallas kernels for 0%

commit v1 on v0

--- a/solution.py
+++ b/solution.py
@@ -56,7 +56,8 @@
     grad_k = empty_kv
     grad_v = empty_kv
     key_part = lax.all_gather(key_rows, "seq", axis=1, tiled=True)
-    value_part = lax.all_gather(value_rows, "seq", axis=1, tiled=True)
+    sites_mix = lambda v0: jnp.concatenate(lax.all_gather(v0, axis_name="seq"), axis=1)
+    value_part = sites_mix(value_rows)
     count = key_part.shape[1]
     for begin in range(0, count, width):
         finish = min(begin + width, count)

time: 278 us -> 279 us (level)
  waiting for transfers between devices: 178 us -> 171 us
  local copies, waits for them, and re-layouts: 35.5 us -> 39.3 us
    all_gather x1, waiting for transfers between devices: 24.1 us -> 17.3 us  [local(): lax.all_gather(value_sum.astype(jnp.bfloat16), 'seq', axis=0, tiled=True)]
    unnamed x29 -> x26, local copies, waits for them, and re-layouts: 15.3 us -> 18.9 us
  transfers between devices with their start and end apart: 7 -> 7, of which waited for: 6 -> 6; matrix products, arithmetic and copies ran while one was open for 18% -> 21% of each run, Pallas kernels for 0% -> 0%
where the time goes in v1:
time: 279 us; the launch traced here: 278 us
  waiting for transfers between devices  171 us (61%)
  local copies, waits for them, and re-layouts  39.3 us (14%)
  matrix products  26.8 us (10%)
  between operations  14.9 us (5%)
  other arithmetic  11.3 us (4%)
  blocking collectives  9.51 us (3%)
  starting transfers between devices  4.68 us (2%)
    reduce_scatter x1, waiting for transfers between devices, local(): lax.psum_scatter(part_key.astype(jnp.bfloat16), 'seq', scatter_dimension=...  41.3 us
    unnamed x7, waiting for transfers between devices  41.2 us
    psum x1, waiting for transfers between devices, local(): lax.psum(rows_total.astype(jnp.bfloat16), 'batch').astype(jnp.float32)  35.4 us
    all_gather x1, waiting for transfers between devices, local(): lax.all_gather(v0, axis_name='seq')  19.1 us
    unnamed x26, local copies, waits for them, and re-layouts  18.9 us
    all_gather x1, waiting for transfers between devices, local(): lax.all_gather(value_sum.astype(jnp.bfloat16), 'seq', axis=0, tiled=True)  17.3 us
    all_gather x1, waiting for transfers between devices, local(): key_part = lax.all_gather(key_rows, 'seq', axis=1, tiled=True)  16.8 us
    unnamed x1, blocking collectives  9.51 us
  transfers between devices with their start and end apart: 7, of which 6 were waited for; matrix products, arithmetic and copies ran while one was open for 21% of the time, Pallas kernels for 0%

profile of v1, /device:TPU:0, one launch (start us, length us, event | category | flops | bytes accessed | tf_op | source)
XLA Modules:
  0.0 277.6 jit_solution(2072631305019797407)
XLA Ops:
  11.7 9.5 %all-reduce = s32[8]{0:T(128)S(1)} all-reduce(s32[8]{0:T(128)S(1)} %bitcast_dynamic-update-slice_fusion), channel_id=1, replica_groups=mesh['seq'=8,'batch'=4] {'seq'}, use_global_device_ids=true, to_apply=%add | all-reduce | flops 8 | bytes 64
  24.5 16.8 %all-gather.5.cloned.1.call-done = bf16[1,1024,1024]{1,2,0:T(8,128)(2,1)} async-done(((bf16[1,128,1024]{1,2,0:T(8,128)(2,1)}), bf16[1,1024,1024]{1,2,0:T(8,128)(2,1)}) %all-gather.5.cloned.1.call-update) | async-done | bytes 2097168 | tf_op jit(solution)/shard_map/all_gather | solution.py:58
  49.6 3.9 %copy.108 = bf16[1024,1024]{1,0:T(8,128)(2,1)} copy(bf16[1024,1024]{0,1:T(8,128)(2,1)} %pad_maximum_fusion.1) | data formatting | bytes 4194304
  54.3 40.5 %reduce-scatter.7.cloned.1.call-done = bf16[128,1024]{1,0:T(8,128)(2,1)} async-done(((bf16[1024,1024]{1,0:T(8,128)(2,1)}), bf16[128,1024]{1,0:T(8,128)(2,1)}) %reduce-scatter.7.cloned.1.call-update) | async-done | bytes 262160
  96.6 2.4 copy.81
  99.0 4.3 %all-to-all-start = ((bf16[128,8,576]{0,2,1:T(8,128)(2,1)}), bf16[128,8,576]{0,2,1:T(8,128)(2,1)}, u32[]{:S(2)}, u32[]{:S(2)}) async-start(bf16[128,8,576]{0,2,1:T(8,128)(2,1)} %bitcast.147), calls=%async_computation.1 | async-start | bytes 2359296 | tf_op jit(solution)/shard_map/all_to_all | solution.py:86
  103.5 3.1 %reshape.108 = f32[128,8,2,128]{3,2,1,0:T(2,128)} reshape(bf16[1,128,2048]{2,1,0:T(8,128)(2,1)} %param.11) | data formatting | bytes 1572864 | tf_op jit(solution)/shard_map/convert_element_type | solution.py:46
  106.6 3.2 %multiply_reduce_fusion = f32[128,8,2]{2,1,0:T(8,128)} fusion(f32[128,8,2,128]{3,2,1,0:T(2,128)} %reshape.108, bf16[128,8,2,128]{3,2,1,0:T(2,128)(2,1)S(1)} %reshape_squeeze.22), kind=kLoop, calls=%fused_computation.37 | loop fusion | flops 784384 | bytes 1581056 | tf_op jit(solution)/shard_map/reduce_sum | solution.py:46
  111.0 19.1 %all-gather.9.cloned.1.call-done = bf16[8,128,1024]{2,1,0:T(8,128)(2,1)} async-done(((bf16[1,128,1024]{2,1,0:T(8,128)(2,1)}), bf16[8,128,1024]{2,1,0:T(8,128)(2,1)}) %all-gather.9.cloned.1.call-update) | async-done | bytes 2097168 | tf_op jit(solution)/shard_map/all_gather | solution.py:59
  130.1 3.0 %fusion.35 = (bf16[1,512,1024]{2,1,0:T(8,128)(2,1)}, bf16[1,512,1024]{2,1,0:T(8,128)(2,1)}) fusion(bf16[1,1024,1024]{2,1,0:T(8,128)(2,1)} %bitcast.151), kind=kLoop, calls=%fused_computation.50 | loop fusion | bytes 4194304 | tf_op jit(solution)/shard_map/slice | solution.py:69
  133.2 2.3 copy.111
  135.5 2.3 copy.110
  137.8 5.5 %fusion.1 = bf16[8,2,128,512]{2,3,1,0:T(8,128)(2,1)} fusion(f32[8,512,128,2]{2,1,3,0:T(8,128)} %copy-done.3, bf16[512,8,128,1]{0,2,3,1:T(8,128)(2,1)} %bitcast.156, bf16[128,8,2,128]{0,3,2,1:T(8,128)(2,1)S(1)} %copy-done.6, f32[8,2,128]{2,1,0:T(2,128)S(1)} %copy.63, f32[8,2,128]{2,1,0:T(2,128)S(1)} %bitcast.163, pred[128,512]{0,1:T(8,128)(4,1)S(1)} %get-tuple-element.16), kind=kOutput, calls=%fused_computation.3 | convolution fusion | flops 274726912 | bytes 7946240 | tf_op jit(solution)/shard_map/tgrd,kgd->grtk/dot_general | solution.py:19
  143.3 17.3 %all-gather.7.cloned.1.call-done = bf16[1024,1024]{0,1:T(8,128)(2,1)} async-done(((bf16[128,1024]{0,1:T(8,128)(2,1)}), bf16[1024,1024]{0,1:T(8,128)(2,1)}) %all-gather.7.cloned.1.call-update) | async-done | bytes 2097168 | tf_op jit(solution)/shard_map/all_gather | solution.py:85
  160.6 3.9 %copy.80 = bf16[1024,1024]{1,0:T(8,128)(2,1)} copy(bf16[1024,1024]{0,1:T(8,128)(2,1)} %all-gather.7.cloned.1.call-done) | data formatting | bytes 4194304 | tf_op jit(solution)/shard_map/all_gather | solution.py:85
  164.5 5.9 %convert_reduce_fusion = bf16[1024,576]{0,1:T(8,128)(2,1)} fusion(bf16[8,128,1024]{2,1,0:T(8,128)(2,1)} %bitcast.152, bf16[128,8,576]{0,2,1:T(8,128)(2,1)} %all-to-all-done), kind=kOutput, calls=%fused_computation | convolution fusion | flops 1216806912 | bytes 4456448 | tf_op jit(solution)/shard_map/std,stk->sdk/dot_general | solution.py:88
  170.4 3.4 %fusion.14 = bf16[8,512,128]{1,2,0:T(8,128)(2,1)} fusion(bf16[8,2,128,512]{2,3,1,0:T(8,128)(2,1)} %fusion.1, bf16[128,8,2,128]{0,3,2,1:T(8,128)(2,1)S(1)} %bitcast.141), kind=kOutput, calls=%fused_computation.22 | convolution fusion | flops 269484032 | bytes 3670016 | tf_op jit(solution)/shard_map/grtk,tgrd->kgd/dot_general | solution.py:26
  173.8 2.3 copy.75
  176.1 4.0 %fusion.5 = bf16[8,2,128,512]{2,3,1,0:T(8,128)(2,1)S(1)} fusion(f32[8,512,128,2]{2,1,3,0:T(8,128)} %copy-done.2, bf16[512,8,128,1]{0,2,3,1:T(8,128)(2,1)} %bitcast.155, bf16[128,8,2,128]{0,3,2,1:T(8,128)(2,1)S(1)} %copy-done.6, f32[8,2,128]{2,1,0:T(2,128)S(1)} %copy.63, f32[8,2,128]{2,1,0:T(2,128)S(1)} %bitcast.164, pred[128,512]{0,1:T(8,128)(4,1)S(1)} %get-tuple-element.17), kind=kOutput, calls=%fused_computation.9 | convolution fusion | flops 274726912 | bytes 7946240 | tf_op jit(solution)/shard_map/tgrd,kgd->grtk/dot_general | solution.py:19
  181.9 2.3 copy.74
  184.1 3.1 %pad_maximum_fusion = bf16[1024,1024]{1,0:T(8,128)(2,1)} fusion(bf16[512,1024]{1,0:T(8,128)(2,1)} %copy.75, bf16[512,1024]{1,0:T(8,128)(2,1)} %copy.74), kind=kLoop, calls=%fused_computation.17 | loop fusion | flops 4194304 | bytes 4194304 | tf_op jit(solution)/shard_map/dynamic_update_slice | solution.py:74
  191.1 35.4 %all-reduce.3.cloned.1.call-done = bf16[576,1024]{1,0:T(8,128)(2,1)} async-done(((bf16[576,1024]{1,0:T(8,128)(2,1)}), bf16[576,1024]{1,0:T(8,128)(2,1)}) %all-reduce.3.cloned.1.call-update) | async-done | bytes 1179664 | tf_op jit(solution)/shard_map/psum | solution.py:95
  226.5 3.0 %convert_element_type.60 = f32[576,1024]{1,0:T(8,128)} convert(bf16[576,1024]{1,0:T(8,128)(2,1)} %all-reduce.3.cloned.1.call-done) | non-fusion elementwise | flops 589824 | bytes 3538944 | tf_op jit(solution)/shard_map/convert_element_type | solution.py:95
  229.5 41.3 %reduce-scatter.5.cloned.1.call-done = bf16[128,1024]{1,0:T(8,128)(2,1)} async-done(((bf16[1024,1024]{1,0:T(8,128)(2,1)}), bf16[128,1024]{1,0:T(8,128)(2,1)}) %reduce-scatter.5.cloned.1.call-update) | async-done | bytes 262160 | tf_op jit(solution)/shard_map/reduce_scatter | solution.py:78
  (52 shorter events, 25.0 us)
Async XLA Ops:
  7.2 16.6 %copy-start.4 = (bf16[1,128,2048]{2,1,0:T(8,128)(2,1)S(1)}, bf16[1,128,2048]{2,1,0:T(8,128)(2,1)}, u32[]{:S(2)}) copy-start(bf16[1,128,2048]{2,1,0:T(8,128)(2,1)} %param.8) | copy-start | bytes 1572868
  7.2 34.1 %all-gather.5.cloned.1.call-start = ((), (), s32[]{:S(2)}) async-start(), calls=%async_computation.3 | async-start | bytes 2359296 | tf_op jit(solution)/shard_map/all_gather | solution.py:58
  9.1 85.7 %reduce-scatter.7.cloned.1.call-start = ((), (), s32[]{:S(2)}) async-start(), calls=%async_computation.8 | async-start | bytes 2359296
  43.7 2.0 copy-start.3
  43.8 2.0 copy-start.5
  43.8 1.9 copy-start.7
  44.5 2.4 copy-start.2
  53.5 76.6 %all-gather.9.cloned.1.call-start = ((), (), s32[]{:S(2)}) async-start(), calls=%async_computation.7 | async-start | bytes 2359296 | tf_op jit(solution)/shard_map/all_gather | solution.py:59
  54.3 106.3 %all-gather.7.cloned.1.call-start = ((), (), s32[]{:S(2)}) async-start(), calls=%async_computation.5 | async-start | bytes 2359296 | tf_op jit(solution)/shard_map/all_gather | solution.py:85
  99.0 65.5 %all-to-all-start = ((bf16[128,8,576]{0,2,1:T(8,128)(2,1)}), bf16[128,8,576]{0,2,1:T(8,128)(2,1)}, u32[]{:S(2)}, u32[]{:S(2)}) async-start(bf16[128,8,576]{0,2,1:T(8,128)(2,1)} %bitcast.147), calls=%async_computation.1 | async-start | bytes 2359296 | tf_op jit(solution)/shard_map/all_to_all | solution.py:86
  103.3 123.2 %all-reduce.3.cloned.1.call-start = ((), (), s32[]{:S(2)}) async-start(), calls=%async_computation.6 | async-start | bytes 2359296 | tf_op jit(solution)/shard_map/psum | solution.py:95
  133.2 4.6 %copy-start.6 = (bf16[128,8,2,128]{0,3,2,1:T(8,128)(2,1)S(1)}, bf16[128,8,2,128]{0,3,2,1:T(8,128)(2,1)}, u32[]{:S(2)}) copy-start(bf16[128,8,2,128]{0,3,2,1:T(8,128)(2,1)} %copy.77) | copy-start | bytes 1572868
  170.4 100.4 %reduce-scatter.5.cloned.1.call-start = ((), (), s32[]{:S(2)}) async-start(), calls=%async_computation.4 | async-start | bytes 2359296 | tf_op jit(solution)/shard_map/reduce_scatter | solution.py:78
  180.1 1.8 copy-start.1
  187.2 2.3 copy-start
Sparse Core Ops, SparseCore 0:
  10.4 30.8 all-gather.4
  53.7 41.0 reduce-scatter.6
  96.7 33.3 all-gather.8
  132.4 28.0 all-gather.6
  170.5 55.9 all-reduce.2
  230.2 40.5 reduce-scatter.4
